TPU v7x, 256 devices: a whole 4x4x8 slice. The times are simulated.
256 devices in a mesh: expert: 32 (over z_hi, y, core), dp: 8 (over z_lo, x).
Axes of the slice: x: 4, y: 4, z: 8 (z_hi: 4, z_lo: 2; z = z_hi * 2 + z_lo), core: 2. Of those that a mesh axis runs over, the one named last changes fastest.
Arguments:
- tokens: bfloat16 [32768, 4096], P(('expert', 'dp')), may hold values from -6 to 6
- route: int32 [32768, 2], P(('expert', 'dp')), may hold values from 0 to 63, all different within a row; in each aligned block of 128 rows (0 to 127, 128 to 255, ...) at most 12 rows name the same one
- gate_output_gradient: bfloat16 [32768, 2, 1536], P(('expert', 'dp')), may hold values from -0.4375 to 0.4375
- frozen_gate_weight: bfloat16 [64, 4096, 1536], P('expert', 'dp'), may hold values from -0.09375 to 0.09375
- adapter_first: bfloat16 [64, 4096, 16], P('expert'), may hold values from -0.09375 to 0.09375
- adapter_second: bfloat16 [64, 16, 1536], P('expert'), may hold values from -0.15625 to 0.15625
Outputs:
- grad_a: float32 [64, 4096, 16], P('expert')
- grad_b: float32 [64, 16, 1536], P('expert')
Inputs may be any that keep to these rules, and one draw needn't show every extreme that they name: `route`: each row names 2 different experts. Within each device's aligned block of 128 rows no expert is named more than 12 times.
All inputs are finite; a program needn't handle non-finite values.
Results may differ from a plain program's by a relative error of at most 0.0043.
Values may be sent and summed in bfloat16 or wider, within the bound.
No kernel may reach another device: no remote copies, remote signals or barrier semaphores. Data moves between devices by JAX's collectives and lax.ppermute only.
A program may use at most 128 MiB of HBM per device.

v0:
```python
import jax
import jax.numpy as jnp
from jax import lax
from jax.sharding import PartitionSpec as P

ADAPTER_SCALE = 2.0


def silu_slope(gate_preactivation):
    squash = jax.nn.sigmoid(gate_preactivation)
    return squash * (1.0 + gate_preactivation * (1.0 - squash))


def block_product(input_rows, piece):
    return jnp.dot(input_rows, piece, preferred_element_type=jnp.float32)


def prepare(input_rows, rows_g):
    block = 128
    return (input_rows, rows_g, None, block)


def adapter_grads(input_rows, rows_g, frozen_output, first_adapter_factor, second_adapter_factor):
    rank_reduced_output = jnp.dot(
        input_rows, first_adapter_factor, preferred_element_type=jnp.float32
    ).astype(jnp.bfloat16)
    gate_preactivation = frozen_output + ADAPTER_SCALE * jnp.dot(
        rank_reduced_output, second_adapter_factor, preferred_element_type=jnp.float32
    )
    activation_slope = (rows_g.astype(jnp.float32) * silu_slope(gate_preactivation)).astype(
        jnp.bfloat16
    )
    up_gradient = ADAPTER_SCALE * jnp.einsum(
        "nr,nf->rf", rank_reduced_output, activation_slope, preferred_element_type=jnp.float32
    )
    rank_backward = jnp.einsum(
        "nf,rf->nr", activation_slope, second_adapter_factor, preferred_element_type=jnp.float32
    ).astype(jnp.bfloat16)
    down_gradient = ADAPTER_SCALE * jnp.einsum(
        "nd,nr->dr", input_rows, rank_backward, preferred_element_type=jnp.float32
    )
    return (down_gradient, up_gradient)


def local(tokens, route, gate_output_gradient, frozen_gate_weight, adapter_first, adapter_second):
    experts_here = frozen_gate_weight.shape[0]
    columns = lax.axis_size("expert")
    experts = experts_here * columns
    tok_rows = tokens.shape[0]
    top_count = route.shape[1]
    width = tokens.shape[1]
    hidden = gate_output_gradient.shape[2]
    capacity = 3 * tok_rows * top_count // experts
    slot_count = tok_rows * top_count
    flat_route = route.reshape(slot_count)
    labels = jnp.arange(experts, dtype=jnp.int32)
    one_hot = (flat_route[:, None] == labels[None, :]).astype(jnp.int32)
    ranks = jnp.sum((jnp.cumsum(one_hot, axis=0) - one_hot) * one_hot, axis=1)
    target = (flat_route % experts_here * columns + flat_route // experts_here) * capacity + ranks
    positions = jnp.arange(experts * capacity, dtype=jnp.int32)
    hits = target[None, :] == positions[:, None]
    filled = jnp.any(hits, axis=1)
    slot_ids = jnp.arange(slot_count, dtype=jnp.int32)
    source_slot = jnp.sum(jnp.where(hits, slot_ids[None, :], 0), axis=1)
    send_x = tokens[source_slot // top_count].reshape(experts_here, columns, capacity, width)
    flat_grad = gate_output_gradient.reshape(slot_count, hidden)
    send_g = jnp.where(
        filled[:, None], flat_grad[source_slot], jnp.zeros((), gate_output_gradient.dtype)
    )
    send_g = send_g.reshape(experts_here, columns, capacity, hidden)
    group_rows = columns * capacity
    recv_x, recv_g = (
        lax.all_to_all(send_x, "expert", split_axis=1, concat_axis=1, tiled=True),
        lax.all_to_all(send_g, "expert", split_axis=1, concat_axis=1, tiled=True),
    )
    input_rows = recv_x.reshape(experts_here, group_rows, width)
    rows_g = recv_g.reshape(experts_here, group_rows, hidden)
    ready_inputs = [
        prepare(input_rows[local_result], rows_g[local_result])
        for local_result in range(experts_here)
    ]

    def add_rows(piece):
        return jnp.stack(
            [
                block_product(ready_inputs[local_result][0], piece[local_result])
                for local_result in range(experts_here)
            ]
        )

    frozen_output = add_rows(lax.all_gather(frozen_gate_weight, "dp", axis=1, tiled=True))
    results = [
        adapter_grads(
            ready_inputs[local_result][0],
            ready_inputs[local_result][1],
            frozen_output[local_result],
            adapter_first[local_result],
            adapter_second[local_result],
        )
        for local_result in range(experts_here)
    ]
    grad_a_local = jnp.stack([result[0] for result in results])
    grad_b_local = jnp.stack([result[1] for result in results])
    grad_a, grad_b = lax.psum((grad_a_local, grad_b_local), "dp")
    return (grad_a, grad_b)


def solution(mesh):
    return jax.shard_map(
        local,
        mesh=mesh,
        in_specs=(
            P(("expert", "dp"), None),
            P(("expert", "dp"), None),
            P(("expert", "dp"), None, None),
            P("expert", "dp", None),
            P("expert", None, None),
            P("expert", None, None),
        ),
        out_specs=(P("expert", None, None), P("expert", None, None)),
        check_vma=False,
    )
```

profile of v0, /device:TPU:8, one launch (start us, length us, event | category | flops | bytes accessed | tf_op | source)
XLA Modules:
  0.0 568.3 jit_solution(11198235258273988007)
XLA Ops:
  7.2 0.0 copy-start
  7.2 0.0 copy-start.8
  7.2 0.0 copy-start.5
  7.2 0.0 all-gather.2.cloned.1.call-start
  7.2 0.7 all-gather.2.cloned.1.call-update
  7.9 0.0 copy-done.8
  7.9 0.1 copy.16
  8.1 0.1 eq.41
  8.2 0.1 reshape.174
  8.4 0.6 reduce-window.6
  9.0 0.2 slice_reduce_fusion.2
  9.2 0.0 copy-done.5
  9.2 0.3 reshape.177
  9.5 0.1 fusion.17
  9.6 0.2 select_reduce_fusion
  9.9 3.9 gather_fusion.1
  13.7 4.8 gather.10
  18.5 0.2 fusion.10
  18.7 0.1 broadcast_in_dim.35
  18.8 2.2 broadcast_select_fusion
  21.0 3.8 copy.20
  24.8 11.7 %all-to-all-start.1 = ((bf16[2,32,12,1536]{3,0,2,1:T(2,128)(2,1)}), bf16[2,32,12,1536]{3,0,2,1:T(2,128)(2,1)S(1)}, u32[]{:S(2)}, u32[]{:S(2)}) async-start(bf16[2,32,12,1536]{3,0,2,1:T(2,128)(2,1)} %copy.20), calls=%async_computation.1 | async-start | bytes 4718592 | tf_op jit(solution)/shard_map/all_to_all | solution.py:74
  36.6 0.0 copy-done
  36.6 5.7 gather_fusion
  42.2 9.8 %reshape.176 = bf16[2,32,12,4096]{3,2,1,0:T(8,128)(2,1)} reshape(bf16[768,4096]{1,0:T(8,128)(2,1)} %gather_fusion) | data formatting | bytes 12582912 | tf_op jit(solution)/shard_map/reshape | solution.py:65
  52.0 13.6 %copy.19 = bf16[2,32,12,4096]{3,0,2,1:T(2,128)(2,1)} copy(bf16[2,32,12,4096]{3,2,1,0:T(8,128)(2,1)} %reshape.176) | data formatting | bytes 12582912 | tf_op jit(solution)/shard_map/reshape | solution.py:65
  65.5 53.0 %all-to-all-done.1 = bf16[2,32,12,1536]{3,0,2,1:T(2,128)(2,1)S(1)} async-done(((bf16[2,32,12,1536]{3,0,2,1:T(2,128)(2,1)}), bf16[2,32,12,1536]{3,0,2,1:T(2,128)(2,1)S(1)}, u32[]{:S(2)}, u32[]{:S(2)}) %all-to-all-start.1) | async-done | bytes 2359328 | tf_op jit(solution)/shard_map/all_to_all | solution.py:74
  118.6 5.3 all-to-all-start
  123.9 0.0 all-reduce.3.cloned.1.call-start
  124.0 15.2 %fusion.7 = (f32[32,12,1536]{2,1,0:T(8,128)}, f32[32,12,1536]{2,1,0:T(8,128)}) fusion(bf16[2,32,12,1536]{3,0,2,1:T(2,128)(2,1)S(1)} %all-to-all-done.1), kind=kLoop, calls=%fused_computation.20 | loop fusion | flops 1179648 | bytes 7077888 | tf_op jit(solution)/shard_map/convert_element_type | solution.py:30
  139.1 3.6 reshape.178
  142.7 3.6 reshape.179
  146.2 186.4 %all-to-all-done = bf16[2,32,12,4096]{3,0,2,1:T(2,128)(2,1)} async-done(((bf16[2,32,12,4096]{3,0,2,1:T(2,128)(2,1)}), bf16[2,32,12,4096]{3,0,2,1:T(2,128)(2,1)}, u32[]{:S(2)}, u32[]{:S(2)}) %all-to-all-start) | async-done | bytes 6291488 | tf_op jit(solution)/shard_map/all_to_all | solution.py:73
  332.6 33.0 %slice_reduce_fusion.1 = (bf16[32,12,4096]{2,1,0:T(8,128)(2,1)}, bf16[32,12,4096]{2,1,0:T(8,128)(2,1)}) fusion(bf16[2,32,12,4096]{3,0,2,1:T(2,128)(2,1)} %all-to-all-done), kind=kLoop, calls=%fused_computation.7 | loop fusion | bytes 12582912 | tf_op jit(solution)/shard_map/slice | solution.py:79
  365.6 5.6 squeeze.26
  371.2 0.0 copy-start.6
  371.2 5.6 squeeze.30
  376.8 0.0 copy-done.6
  376.8 0.0 copy-start.2
  376.8 3.0 convolution_convert_fusion.3
  379.8 0.0 copy-done.2
  379.8 0.9 convolution_convert_fusion.1
  380.8 0.0 copy-start.7
  380.8 69.1 %all-gather.2.cloned.1.call-done = bf16[2,4096,1536]{2,1,0:T(8,128)(2,1)} async-done(((bf16[2,512,1536]{2,1,0:T(8,128)(2,1)}), bf16[2,4096,1536]{2,1,0:T(8,128)(2,1)}) %all-gather.2.cloned.1.call-update) | async-done | bytes 25165840 | tf_op jit(solution)/shard_map/all_gather | solution.py:91
  449.8 0.0 copy-start.4
  449.8 9.3 %fusion.1 = f32[384,1536]{1,0:T(8,128)S(1)} fusion(bf16[384,4096]{1,0:T(8,128)(2,1)} %squeeze.26, bf16[2,4096,1536]{2,1,0:T(8,128)(2,1)} %all-gather.2.cloned.1.call-done), kind=kOutput, calls=%fused_computation.5 | convolution fusion | flops 4831838208 | bytes 18087936 | tf_op jit(solution)/shard_map/dot_general | solution.py:15
  459.1 0.0 copy-done.7
  459.2 0.0 copy-done.4
  459.2 1.1 multiply_convert_fusion.1
  460.3 0.3 fusion.8
  460.6 3.0 fusion.3
  463.6 0.0 copy-start.3
  463.6 9.1 %fusion = f32[384,1536]{1,0:T(8,128)S(1)} fusion(bf16[384,4096]{1,0:T(8,128)(2,1)} %squeeze.30, bf16[2,4096,1536]{2,1,0:T(8,128)(2,1)} %all-gather.2.cloned.1.call-done), kind=kOutput, calls=%fused_computation.3 | convolution fusion | flops 4831838208 | bytes 18087936 | tf_op jit(solution)/shard_map/dot_general | solution.py:15
  472.7 0.0 copy-done.3
  472.7 1.1 multiply_convert_fusion
  473.8 0.3 fusion.9
  474.1 3.1 fusion.2
  477.2 0.7 pad_maximum_fusion.1
  477.9 0.8 pad_maximum_fusion
  478.7 0.0 all-reduce.3.cloned.1.call-update
  478.7 79.3 %all-reduce.3.cloned.1.call-done = (f32[2,4096,16]{1,2,0:T(8,128)}, f32[2,16,1536]{2,1,0:T(8,128)}) async-done(((f32[2,4096,16]{1,2,0:T(8,128)}, f32[2,16,1536]{2,1,0:T(8,128)}), (f32[2,4096,16]{1,2,0:T(8,128)}, f32[2,16,1536]{2,1,0:T(8,128)})) %all-reduce.3.cloned.1.call-update) | async-done | bytes 720912 | tf_op jit(solution)/shard_map/psum | solution.py:104
  558.0 1.9 copy.29
  559.9 1.6 copy.30
  561.5 0.0 copy-done.1
  (7 shorter events, 0.1 us)
Async XLA Ops:
  7.2 29.4 %copy-start = (bf16[128,4096]{1,0:T(8,128)(2,1)S(1)}, bf16[128,4096]{1,0:T(8,128)(2,1)}, u32[]{:S(2)}) copy-start(bf16[128,4096]{1,0:T(8,128)(2,1)} %param.6) | copy-start | bytes 3145732
  7.2 0.8 copy-start.8
  7.2 2.0 copy-start.5
  7.2 442.6 %all-gather.2.cloned.1.call-start = ((), (), s32[]{:S(2)}) async-start(), calls=%async_computation.2 | async-start | bytes 28311552 | tf_op jit(solution)/shard_map/all_gather | solution.py:91
  24.8 93.7 %all-to-all-start.1 = ((bf16[2,32,12,1536]{3,0,2,1:T(2,128)(2,1)}), bf16[2,32,12,1536]{3,0,2,1:T(2,128)(2,1)S(1)}, u32[]{:S(2)}, u32[]{:S(2)}) async-start(bf16[2,32,12,1536]{3,0,2,1:T(2,128)(2,1)} %copy.20), calls=%async_computation.1 | async-start | bytes 4718592 | tf_op jit(solution)/shard_map/all_to_all | solution.py:74
  118.6 214.0 %all-to-all-start = ((bf16[2,32,12,4096]{3,0,2,1:T(2,128)(2,1)}), bf16[2,32,12,4096]{3,0,2,1:T(2,128)(2,1)}, u32[]{:S(2)}, u32[]{:S(2)}) async-start(bf16[2,32,12,4096]{3,0,2,1:T(2,128)(2,1)} %copy.19), calls=%async_computation | async-start | bytes 12582912 | tf_op jit(solution)/shard_map/all_to_all | solution.py:73
  123.9 434.1 %all-reduce.3.cloned.1.call-start = ((), (), s32[]{:S(2)}) async-start(), calls=%async_computation.3 | async-start | bytes 1441792 | tf_op jit(solution)/shard_map/psum | solution.py:104
  371.2 5.6 copy-start.6
  376.8 3.0 copy-start.2
  380.8 78.4 %copy-start.7 = (bf16[2,16,1536]{2,1,0:T(8,128)(2,1)S(1)}, bf16[2,16,1536]{2,1,0:T(8,128)(2,1)}, u32[]{:S(2)}) copy-start(bf16[2,16,1536]{2,1,0:T(8,128)(2,1)} %param.11) | copy-start | bytes 294916
  449.8 9.3 %copy-start.4 = (f32[384,1536]{1,0:T(8,128)S(1)}, f32[384,1536]{1,0:T(8,128)}, u32[]{:S(2)}) copy-start(f32[384,1536]{1,0:T(8,128)} %reshape.178) | copy-start | bytes 7077892
  463.6 9.1 %copy-start.3 = (f32[384,1536]{1,0:T(8,128)S(1)}, f32[384,1536]{1,0:T(8,128)}, u32[]{:S(2)}) copy-start(f32[384,1536]{1,0:T(8,128)} %reshape.179) | copy-start | bytes 7077892
  474.1 87.4 %copy-start.1 = (bf16[128,4096]{1,0:T(8,128)(2,1)S(1)}, bf16[128,4096]{1,0:T(8,128)(2,1)}, u32[]{:S(2)}) copy-start(bf16[128,4096]{1,0:T(8,128)(2,1)} %param.6) | copy-start | bytes 3145732
Sparse Core Ops, SparseCore 0:
  9.8 439.9 all-gather.1
  478.8 79.1 all-reduce.2
where the time goes:
time: 569 us; the launch traced here: 568 us
  waiting for transfers between devices  388 us (68%)
  local copies, waits for them, and re-layouts  97.3 us (17%)
  matrix products  31.2 us (5%)
  other arithmetic  20 us (4%)
  starting transfers between devices  17.1 us (3%)
  between operations  14.2 us (2%)
    all_to_all x1, waiting for transfers between devices, local(): lax.all_to_all(send_x, 'expert', split_axis=1, concat_axis=1, tiled=True)  186 us
    psum x1, waiting for transfers between devices, local(): grad_a, grad_b = lax.psum((grad_a_local, grad_b_local), 'dp')  79.3 us
    all_gather x1, waiting for transfers between devices, local(): lax.all_gather(frozen_gate_weight, 'dp', axis=1, tiled=True)  69.1 us
    all_to_all x1, waiting for transfers between devices, local(): lax.all_to_all(send_g, 'expert', split_axis=1, concat_axis=1, tiled=True)  53 us
    slice x1, local copies, waits for them, and re-layouts, local(): input_rows[local_result]  33 us
    reshape x2, local copies, waits for them, and re-layouts, local(): tokens[source_slot // top_count]  23.3 us
    dot_general x2, matrix products, block_product(): return jnp.dot(input_rows, piece, preferred_element_type=jnp.float32)  18.4 us
    convert_element_type x1, other arithmetic, adapter_grads(): rows_g.astype(jnp.float32) * silu_slope(gate_preactivation)  15.2 us
  transfers between devices with their start and end apart: 4, of which 4 were waited for; matrix products, arithmetic and copies ran while one was open for 20% of the time, Pallas kernels for 0%

commit v1 on v0

--- a/solution.py
+++ b/solution.py
@@ -88,7 +88,12 @@
             ]
         )
 
-    frozen_output = add_rows(lax.all_gather(frozen_gate_weight, "dp", axis=1, tiled=True))
+    frozen_output = add_rows(
+        jnp.concatenate(
+            lax.all_to_all(jnp.stack([frozen_gate_weight] * lax.axis_size("dp")), "dp", 0, 0),
+            axis=1,
+        )
+    )
     results = [
         adapter_grads(
             ready_inputs[local_result][0],

time: 569 us -> 657 us (1.15)
  blocking collectives: 0 us -> 117 us
  waiting for transfers between devices: 388 us -> 305 us
  starting transfers between devices: 17.1 us -> 50.2 us
  local copies, waits for them, and re-layouts: 97.3 us -> 122 us
    all_to_all x0 -> x1, blocking collectives: none -> 117 us  [local(): lax.all_to_all(send_x, 'expert', split_axis=1, concat_axis=1, tiled=True)]
    all_gather x1 -> x0, waiting for transfers between devices: 69.1 us -> none  [local(): lax.all_gather(frozen_gate_weight, 'dp', axis=1, tiled=True)]
    all_to_all x1, starting transfers between devices: 5.3 us -> 38.2 us  [local(): lax.all_to_all(jnp.stack([frozen_gate_weight] * lax.axis_size('dp')), 'dp...]
    all_to_all x1, waiting for transfers between devices: 53 us -> 23.8 us  [local(): lax.all_to_all(send_g, 'expert', split_axis=1, concat_axis=1, tiled=True)]
    all_to_all x1, waiting for transfers between devices: 186 us -> 202 us  [local(): lax.all_to_all(jnp.stack([frozen_gate_weight] * lax.axis_size('dp')), 'dp...]
    slice x1 -> x2, local copies, waits for them, and re-layouts: 0.18 us -> 14 us  [the longest x1 13.8 us: add_rows(): piece[local_result]]
    another operation x1 -> x2, local copies, waits for them, and re-layouts: 0.01 us -> 8.61 us  [the longest x1 8.61 us: local(): jnp.stack([frozen_gate_weight] * lax.axis_size('dp'))]
  transfers between devices with their start and end apart: 4 -> 3, of which waited for: 4 -> 3; matrix products, arithmetic and copies ran while one was open for 20% -> 15% of each run, Pallas kernels for 0% -> 0%
where the time goes in v1:
time: 657 us; the launch traced here: 656 us
  waiting for transfers between devices  305 us (46%)
  local copies, waits for them, and re-layouts  122 us (19%)
  blocking collectives  117 us (18%)
  starting transfers between devices  50.2 us (8%)
  matrix products  26.9 us (4%)
  other arithmetic  19.9 us (3%)
  between operations  14.2 us (2%)
    all_to_all x1, waiting for transfers between devices, local(): lax.all_to_all(jnp.stack([frozen_gate_weight] * lax.axis_size('dp')), 'dp...  202 us
    all_to_all x1, blocking collectives, local(): lax.all_to_all(send_x, 'expert', split_axis=1, concat_axis=1, tiled=True)  117 us
    psum x1, waiting for transfers between devices, local(): grad_a, grad_b = lax.psum((grad_a_local, grad_b_local), 'dp')  78.7 us
    all_to_all x1, starting transfers between devices, local(): lax.all_to_all(jnp.stack([frozen_gate_weight] * lax.axis_size('dp')), 'dp...  38.2 us
    slice x1, local copies, waits for them, and re-layouts, local(): input_rows[local_result]  32.9 us
    all_to_all x1, waiting for transfers between devices, local(): lax.all_to_all(send_g, 'expert', split_axis=1, concat_axis=1, tiled=True)  23.8 us
    reshape x2, local copies, waits for them, and re-layouts, local(): tokens[source_slot // top_count]  23.3 us
    convert_element_type x1, other arithmetic, adapter_grads(): rows_g.astype(jnp.float32) * silu_slope(gate_preactivation)  15 us
  transfers between devices with their start and end apart: 3, of which 3 were waited for; matrix products, arithmetic and copies ran while one was open for 15% of the time, Pallas kernels for 0%

profile of v1, /device:TPU:8, one launch (start us, length us, event | category | flops | bytes accessed | tf_op | source)
XLA Modules:
  0.0 655.8 jit_solution(7743102896658114524)
XLA Ops:
  7.2 0.0 copy-start
  7.2 0.9 copy.16
  8.1 0.1 reshape.184
  8.2 0.1 eq.41
  8.4 0.6 reduce-window.6
  9.0 0.2 slice_reduce_fusion.2
  9.2 0.1 fusion.15
  9.3 0.2 fusion.8
  9.5 0.2 select_reduce_fusion
  9.7 0.1 broadcast_in_dim.35
  9.9 2.3 reshape.187
  12.2 3.8 gather_fusion.1
  16.0 4.8 gather.10
  20.7 2.2 broadcast_select_fusion
  22.9 3.8 copy.20
  26.7 11.7 %all-to-all-start.1 = ((bf16[2,32,12,1536]{3,0,2,1:T(2,128)(2,1)}), bf16[2,32,12,1536]{3,0,2,1:T(2,128)(2,1)S(1)}, u32[]{:S(2)}, u32[]{:S(2)}) async-start(bf16[2,32,12,1536]{3,0,2,1:T(2,128)(2,1)} %copy.20), calls=%async_computation.1 | async-start | bytes 4718592 | tf_op jit(solution)/shard_map/all_to_all | solution.py:74
  38.4 0.0 copy-done
  38.4 5.8 gather_fusion
  44.2 9.8 %reshape.186 = bf16[2,32,12,4096]{3,2,1,0:T(8,128)(2,1)} reshape(bf16[768,4096]{1,0:T(8,128)(2,1)} %gather_fusion) | data formatting | bytes 12582912 | tf_op jit(solution)/shard_map/reshape | solution.py:65
  54.0 13.6 %copy.19 = bf16[2,32,12,4096]{3,0,2,1:T(2,128)(2,1)} copy(bf16[2,32,12,4096]{3,2,1,0:T(8,128)(2,1)} %reshape.186) | data formatting | bytes 12582912 | tf_op jit(solution)/shard_map/reshape | solution.py:65
  67.6 23.8 %all-to-all-done.1 = bf16[2,32,12,1536]{3,0,2,1:T(2,128)(2,1)S(1)} async-done(((bf16[2,32,12,1536]{3,0,2,1:T(2,128)(2,1)}), bf16[2,32,12,1536]{3,0,2,1:T(2,128)(2,1)S(1)}, u32[]{:S(2)}, u32[]{:S(2)}) %all-to-all-start.1) | async-done | bytes 2359328 | tf_op jit(solution)/shard_map/all_to_all | solution.py:74
  91.4 0.0 copy-start.4
  91.4 117.3 %all_to_all.15 = bf16[2,32,12,4096]{3,0,2,1:T(2,128)(2,1)} all-to-all(bf16[2,32,12,4096]{3,0,2,1:T(2,128)(2,1)} %copy.19), channel_id=1, replica_groups=mesh['expert'=32,'dp'=8] {'expert'}, dimensions={1} | all-to-all | bytes 12582912 | tf_op jit(solution)/shard_map/all_to_all | solution.py:73
  208.7 0.0 copy-done.4
  208.7 8.6 %stack.14 = bf16[8,2,512,1536]{3,2,1,0:T(8,128)(2,1)} broadcast(bf16[2,512,1536]{2,1,0:T(8,128)(2,1)S(1)} %copy-done.4), dimensions={1,2,3} | broadcast | bytes 28311552 | tf_op jit(solution)/shard_map/stack | solution.py:93
  217.3 38.2 %all-to-all-start.2 = ((bf16[8,2,512,1536]{3,2,1,0:T(8,128)(2,1)}), bf16[8,2,512,1536]{3,2,1,0:T(8,128)(2,1)}, u32[]{:S(2)}, u32[]{:S(2)}) async-start(bf16[8,2,512,1536]{3,2,1,0:T(8,128)(2,1)} %stack.14), calls=%async_computation.2 | async-start | bytes 50331648 | tf_op jit(solution)/shard_map/all_to_all | solution.py:93
  255.6 0.2 all-reduce.3.cloned.1.call-start
  255.8 15.0 %fusion.5 = (f32[32,12,1536]{2,1,0:T(8,128)}, f32[32,12,1536]{2,1,0:T(8,128)}) fusion(bf16[2,32,12,1536]{3,0,2,1:T(2,128)(2,1)S(1)} %all-to-all-done.1), kind=kLoop, calls=%fused_computation.16 | loop fusion | flops 1179648 | bytes 7077888 | tf_op jit(solution)/shard_map/convert_element_type | solution.py:30
  270.8 3.6 reshape.189
  274.3 3.6 reshape.190
  277.9 32.9 %slice_reduce_fusion.1 = (bf16[32,12,4096]{2,1,0:T(8,128)(2,1)}, bf16[32,12,4096]{2,1,0:T(8,128)(2,1)}) fusion(bf16[2,32,12,4096]{3,0,2,1:T(2,128)(2,1)} %all_to_all.15), kind=kLoop, calls=%fused_computation.3 | loop fusion | bytes 12582912 | tf_op jit(solution)/shard_map/slice | solution.py:79
  310.8 5.6 squeeze.26
  316.4 0.0 copy-start.7
  316.4 5.6 squeeze.30
  322.0 0.0 copy-done.7
  322.0 0.0 copy-start.2
  322.0 3.0 convolution_convert_fusion.3
  325.0 0.0 copy-done.2
  325.0 0.9 convolution_convert_fusion.1
  325.9 202.4 %all-to-all-done.2 = bf16[8,2,512,1536]{3,2,1,0:T(8,128)(2,1)} async-done(((bf16[8,2,512,1536]{3,2,1,0:T(8,128)(2,1)}), bf16[8,2,512,1536]{3,2,1,0:T(8,128)(2,1)}, u32[]{:S(2)}, u32[]{:S(2)}) %all-to-all-start.2) | async-done | bytes 25165856 | tf_op jit(solution)/shard_map/all_to_all | solution.py:93
  528.3 0.0 copy-start.3
  528.3 13.8 %fusion.33 = (bf16[1,8,512,1536]{3,2,0,1:T(8,128)(2,1)S(1)}, bf16[1,8,512,1536]{3,2,0,1:T(8,128)(2,1)}) fusion(bf16[2,8,512,1536]{3,2,0,1:T(8,128)(2,1)} %bitcast.1), kind=kLoop, calls=%fused_computation.71 | loop fusion | bytes 50331648 | tf_op jit(solution)/shard_map/slice | solution.py:86
  542.1 0.0 copy-done.3
  542.1 0.0 copy-start.6
  542.1 0.0 copy-start.8
  542.1 5.1 fusion.34
  547.2 0.0 copy-done.6
  547.2 0.0 copy-done.8
  547.2 1.1 multiply_convert_fusion.1
  548.3 3.0 fusion.1
  551.3 0.3 fusion.6
  551.6 9.1 %fusion.35 = f32[384,1536]{1,0:T(8,128)S(1)} fusion(bf16[384,4096]{1,0:T(8,128)(2,1)} %squeeze.30, bf16[4096,1536]{1,0:T(8,128)(2,1)} %bitcast.64), kind=kOutput, calls=%fused_computation.73 | convolution fusion | flops 4831838208 | bytes 18087936 | tf_op jit(solution)/shard_map/dot_general | solution.py:15
  560.7 0.0 copy-done.5
  560.7 1.1 multiply_convert_fusion
  561.8 0.0 copy-start.1
  561.8 3.1 fusion
  564.9 0.3 fusion.7
  565.2 0.7 pad_maximum_fusion.1
  565.9 0.8 pad_maximum_fusion
  566.7 0.0 all-reduce.3.cloned.1.call-update
  566.7 78.7 %all-reduce.3.cloned.1.call-done = (f32[2,4096,16]{1,2,0:T(8,128)}, f32[2,16,1536]{2,1,0:T(8,128)}) async-done(((f32[2,4096,16]{1,2,0:T(8,128)}, f32[2,16,1536]{2,1,0:T(8,128)}), (f32[2,4096,16]{1,2,0:T(8,128)}, f32[2,16,1536]{2,1,0:T(8,128)})) %all-reduce.3.cloned.1.call-update) | async-done | bytes 720912 | tf_op jit(solution)/shard_map/psum | solution.py:109
  645.5 1.9 copy.29
  647.3 1.6 copy.30
  649.0 0.0 copy-done.1
  (7 shorter events, 0.1 us)
Async XLA Ops:
  7.2 31.3 %copy-start = (bf16[128,4096]{1,0:T(8,128)(2,1)S(1)}, bf16[128,4096]{1,0:T(8,128)(2,1)}, u32[]{:S(2)}) copy-start(bf16[128,4096]{1,0:T(8,128)(2,1)} %param.6) | copy-start | bytes 3145732
  26.7 64.6 %all-to-all-start.1 = ((bf16[2,32,12,1536]{3,0,2,1:T(2,128)(2,1)}), bf16[2,32,12,1536]{3,0,2,1:T(2,128)(2,1)S(1)}, u32[]{:S(2)}, u32[]{:S(2)}) async-start(bf16[2,32,12,1536]{3,0,2,1:T(2,128)(2,1)} %copy.20), calls=%async_computation.1 | async-start | bytes 4718592 | tf_op jit(solution)/shard_map/all_to_all | solution.py:74
  91.4 117.3 %copy-start.4 = (bf16[2,512,1536]{2,1,0:T(8,128)(2,1)S(1)}, bf16[2,512,1536]{2,1,0:T(8,128)(2,1)}, u32[]{:S(2)}) copy-start(bf16[2,512,1536]{2,1,0:T(8,128)(2,1)} %param.9) | copy-start | bytes 9437188
  217.3 311.0 %all-to-all-start.2 = ((bf16[8,2,512,1536]{3,2,1,0:T(8,128)(2,1)}), bf16[8,2,512,1536]{3,2,1,0:T(8,128)(2,1)}, u32[]{:S(2)}, u32[]{:S(2)}) async-start(bf16[8,2,512,1536]{3,2,1,0:T(8,128)(2,1)} %stack.14), calls=%async_computation.2 | async-start | bytes 50331648 | tf_op jit(solution)/shard_map/all_to_all | solution.py:93
  255.6 389.9 %all-reduce.3.cloned.1.call-start = ((), (), s32[]{:S(2)}) async-start(), calls=%async_computation.3 | async-start | bytes 1441792 | tf_op jit(solution)/shard_map/psum | solution.py:109
  316.4 5.6 copy-start.7
  322.0 3.0 copy-start.2
  528.3 13.8 %copy-start.3 = (bf16[384,4096]{1,0:T(8,128)(2,1)S(1)}, bf16[384,4096]{1,0:T(8,128)(2,1)}, u32[]{:S(2)}) copy-start(bf16[384,4096]{1,0:T(8,128)(2,1)} %squeeze.26) | copy-start | bytes 9437188
  542.1 5.1 copy-start.6
  542.1 5.1 copy-start.8
  551.6 9.1 %copy-start.5 = (f32[384,1536]{1,0:T(8,128)S(1)}, f32[384,1536]{1,0:T(8,128)}, u32[]{:S(2)}) copy-start(f32[384,1536]{1,0:T(8,128)} %reshape.190) | copy-start | bytes 7077892
  561.8 87.1 %copy-start.1 = (bf16[128,4096]{1,0:T(8,128)(2,1)S(1)}, bf16[128,4096]{1,0:T(8,128)(2,1)}, u32[]{:S(2)}) copy-start(bf16[128,4096]{1,0:T(8,128)(2,1)} %param.6) | copy-start | bytes 3145732
Sparse Core Ops, SparseCore 0:
  566.9 78.5 all-reduce.2
